TPU v7x, 16 devices: a whole 2x2x2 slice. The times are simulated.
16 devices in a mesh: rows: 16 (over z, y, x, core).
Axes of the slice: x: 2, y: 2, z: 2, core: 2. Of those that a mesh axis runs over, the one named last changes fastest.
Arguments:
- wave_fn: float32 [256, 4, 4, 256], P('rows')
- left_env: bfloat16 [32, 256, 256], P(None, 'rows')
- op_pair: bfloat16 [32, 16, 16], replicated
- right_env: bfloat16 [32, 256, 256], replicated
Outputs:
- output 1: float32 [7, 256, 4, 4, 256], P(None, 'rows')
- output 2: float32 [6], replicated
- output 3: float32 [6], replicated
All inputs are finite; a program needn't handle non-finite values.
Results may differ from a plain program's by a relative error of at most 0.0116381.
Values are sent between devices in bfloat16 or wider.
A program may use at most 1 GiB of HBM per device.

v0:
```python
import jax
import jax.numpy as jnp
from jax import lax
from jax.sharding import PartitionSpec as P

NUM_STEPS = 6


def solution(mesh):
    row_axis = "rows"

    def local_run(wave_rows, left_rows, op_pair, right_env):
        local_rows = wave_rows.shape[0]
        phys_dim = wave_rows.shape[1]
        bond_dim = wave_rows.shape[3]
        num_terms = left_rows.shape[0]
        pair_dim = phys_dim * phys_dim
        vec_count = bond_dim * bond_dim * pair_dim
        right_flat = jnp.transpose(right_env, (0, 2, 1)).reshape(num_terms * bond_dim, bond_dim)

        def matvec(vec_rows):
            whole_vec = lax.all_gather(vec_rows.astype(jnp.bfloat16), row_axis, axis=0, tiled=True)
            flat_in = whole_vec.reshape(bond_dim, pair_dim * bond_dim)
            left_out = jnp.einsum("kap,pn->kan", left_rows, flat_in, preferred_element_type=jnp.float32)
            left_out = left_out.astype(jnp.bfloat16).reshape(num_terms, local_rows, pair_dim, bond_dim)
            mid_out = jnp.einsum("kqr,karc->aqkc", op_pair, left_out, preferred_element_type=jnp.float32)
            mid_out = mid_out.astype(jnp.bfloat16).reshape(local_rows * pair_dim, num_terms * bond_dim)
            sigma_rows = jnp.dot(mid_out, right_flat, preferred_element_type=jnp.float32)
            return sigma_rows.reshape(local_rows, phys_dim, phys_dim, bond_dim)

        def global_mean(local_val):
            return lax.psum(jnp.sum(local_val), row_axis) / vec_count

        first_vec = wave_rows / jnp.sqrt(global_mean(wave_rows * wave_rows))
        prev_vec = jnp.zeros_like(first_vec)
        cur_vec = first_vec
        beta_prev = jnp.zeros((), jnp.float32)
        vec_list = [first_vec]
        alpha_list = []
        beta_list = []
        for step_idx in range(NUM_STEPS):
            sigma_rows = matvec(cur_vec)
            alpha_val = global_mean(sigma_rows * cur_vec)
            resid_vec = sigma_rows - alpha_val * cur_vec - beta_prev * prev_vec
            beta_val = jnp.sqrt(global_mean(resid_vec * resid_vec))
            next_vec = resid_vec / beta_val
            vec_list.append(next_vec)
            alpha_list.append(alpha_val)
            beta_list.append(beta_val)
            prev_vec = cur_vec
            cur_vec = next_vec
            beta_prev = beta_val
        return jnp.stack(vec_list), jnp.stack(alpha_list), jnp.stack(beta_list)

    return jax.shard_map(local_run, mesh=mesh, in_specs=(P(row_axis), P(None, row_axis), P(), P()), out_specs=(P(None, row_axis), P(), P()), check_vma=False)
```

profile of v0, /device:TPU:0, one launch (start us, length us, event | category | flops | bytes accessed | tf_op | source)
XLA Modules:
  0.0 807.1 jit_solution(14823743407174350208)
XLA Ops:
  9.0 34.7 %psum.91 = f32[]{:T(128)} all-reduce(f32[]{:T(128)} %multiply_reduce_fusion.12), channel_id=1, replica_groups=mesh['rows'=16] {'rows'}, use_global_device_ids=true, to_apply=%region_1.0 | all-reduce | flops 1 | bytes 8 | tf_op jit(solution)/shard_map/psum | solution.py:32
  47.2 6.4 copy.34
  53.6 22.7 %all-gather.7.cloned.1.call-done = bf16[256,4,4,256]{3,0,2,1:T(8,128)(2,1)} async-done(((bf16[16,4,4,256]{3,0,2,1:T(8,128)(2,1)}), bf16[256,4,4,256]{3,0,2,1:T(8,128)(2,1)}) %all-gather.7.cloned.1.call-update) | async-done | bytes 2097168 | tf_op jit(solution)/shard_map/all_gather | solution.py:22
  92.2 7.5 dot_general.68
  99.7 5.4 multiply_reduce_fusion.11
  105.0 32.1 %psum.92 = f32[]{:T(128)} all-reduce(f32[]{:T(128)} %get-tuple-element.21), channel_id=1, replica_groups=mesh['rows'=16] {'rows'}, use_global_device_ids=true, to_apply=%region_3.0 | all-reduce | flops 1 | bytes 8 | tf_op jit(solution)/shard_map/psum | solution.py:32
  138.5 32.7 %psum.93 = f32[]{:T(128)} all-reduce(f32[]{:T(128)} %multiply_reduce_fusion.10), channel_id=1, replica_groups=mesh['rows'=16] {'rows'}, use_global_device_ids=true, to_apply=%region_5.0 | all-reduce | flops 1 | bytes 8 | tf_op jit(solution)/shard_map/psum | solution.py:32
  172.9 30.1 %all-gather.9.cloned.1.call-done = bf16[256,4,4,256]{3,0,2,1:T(8,128)(2,1)} async-done(((bf16[16,4,4,256]{3,0,2,1:T(8,128)(2,1)}), bf16[256,4,4,256]{3,0,2,1:T(8,128)(2,1)}) %all-gather.9.cloned.1.call-update) | async-done | bytes 2097168 | tf_op jit(solution)/shard_map/all_gather | solution.py:22
  217.1 7.4 dot_general.72
  224.5 5.3 multiply_reduce_fusion.9
  229.8 31.9 %psum.94 = f32[]{:T(128)} all-reduce(f32[]{:T(128)} %get-tuple-element.23), channel_id=1, replica_groups=mesh['rows'=16] {'rows'}, use_global_device_ids=true, to_apply=%region_7.0 | all-reduce | flops 1 | bytes 8 | tf_op jit(solution)/shard_map/psum | solution.py:32
  263.1 32.7 %psum.95 = f32[]{:T(128)} all-reduce(f32[]{:T(128)} %get-tuple-element.17), channel_id=1, replica_groups=mesh['rows'=16] {'rows'}, use_global_device_ids=true, to_apply=%region_9.0 | all-reduce | flops 1 | bytes 8 | tf_op jit(solution)/shard_map/psum | solution.py:32
  297.7 29.7 %all-gather.11.cloned.1.call-done = bf16[256,4,4,256]{3,0,2,1:T(8,128)(2,1)} async-done(((bf16[16,4,4,256]{3,0,2,1:T(8,128)(2,1)}), bf16[256,4,4,256]{3,0,2,1:T(8,128)(2,1)}) %all-gather.11.cloned.1.call-update) | async-done | bytes 2097168 | tf_op jit(solution)/shard_map/all_gather | solution.py:22
  341.5 7.4 dot_general.76
  348.9 5.3 multiply_reduce_fusion.7
  354.2 31.9 %psum.96 = f32[]{:T(128)} all-reduce(f32[]{:T(128)} %get-tuple-element.25), channel_id=1, replica_groups=mesh['rows'=16] {'rows'}, use_global_device_ids=true, to_apply=%region_11.0 | all-reduce | flops 1 | bytes 8 | tf_op jit(solution)/shard_map/psum | solution.py:32
  387.4 32.7 %psum.97 = f32[]{:T(128)} all-reduce(f32[]{:T(128)} %get-tuple-element.15), channel_id=1, replica_groups=mesh['rows'=16] {'rows'}, use_global_device_ids=true, to_apply=%region_13.0 | all-reduce | flops 1 | bytes 8 | tf_op jit(solution)/shard_map/psum | solution.py:32
  421.8 29.9 %all-gather.13.cloned.1.call-done = bf16[256,4,4,256]{3,0,2,1:T(8,128)(2,1)} async-done(((bf16[16,4,4,256]{3,0,2,1:T(8,128)(2,1)}), bf16[256,4,4,256]{3,0,2,1:T(8,128)(2,1)}) %all-gather.13.cloned.1.call-update) | async-done | bytes 2097168 | tf_op jit(solution)/shard_map/all_gather | solution.py:22
  465.8 7.4 dot_general.80
  473.2 5.3 multiply_reduce_fusion.5
  478.5 31.9 %psum.98 = f32[]{:T(128)} all-reduce(f32[]{:T(128)} %get-tuple-element.27), channel_id=1, replica_groups=mesh['rows'=16] {'rows'}, use_global_device_ids=true, to_apply=%region_15.0 | all-reduce | flops 1 | bytes 8 | tf_op jit(solution)/shard_map/psum | solution.py:32
  511.7 32.7 %psum.99 = f32[]{:T(128)} all-reduce(f32[]{:T(128)} %get-tuple-element.13), channel_id=1, replica_groups=mesh['rows'=16] {'rows'}, use_global_device_ids=true, to_apply=%region_17.0 | all-reduce | flops 1 | bytes 8 | tf_op jit(solution)/shard_map/psum | solution.py:32
  546.1 29.9 %all-gather.15.cloned.1.call-done = bf16[256,4,4,256]{3,0,2,1:T(8,128)(2,1)} async-done(((bf16[16,4,4,256]{3,0,2,1:T(8,128)(2,1)}), bf16[256,4,4,256]{3,0,2,1:T(8,128)(2,1)}) %all-gather.15.cloned.1.call-update) | async-done | bytes 2097168 | tf_op jit(solution)/shard_map/all_gather | solution.py:22
  590.1 7.4 dot_general.84
  597.5 5.3 multiply_reduce_fusion.3
  602.8 31.9 %psum.100 = f32[]{:T(128)} all-reduce(f32[]{:T(128)} %get-tuple-element.29), channel_id=1, replica_groups=mesh['rows'=16] {'rows'}, use_global_device_ids=true, to_apply=%region_19.0 | all-reduce | flops 1 | bytes 8 | tf_op jit(solution)/shard_map/psum | solution.py:32
  636.0 33.0 %psum.101 = f32[]{:T(128)} all-reduce(f32[]{:T(128)} %get-tuple-element.11), channel_id=1, replica_groups=mesh['rows'=16] {'rows'}, use_global_device_ids=true, to_apply=%region_21.0 | all-reduce | flops 1 | bytes 8 | tf_op jit(solution)/shard_map/psum | solution.py:32
  674.9 25.6 %all-gather.17.cloned.1.call-done = bf16[256,4,4,256]{3,0,2,1:T(8,128)(2,1)} async-done(((bf16[16,4,4,256]{3,0,2,1:T(8,128)(2,1)}), bf16[256,4,4,256]{3,0,2,1:T(8,128)(2,1)}) %all-gather.17.cloned.1.call-update) | async-done | bytes 2097168 | tf_op jit(solution)/shard_map/all_gather | solution.py:22
  714.6 7.4 dot_general.88
  722.0 5.3 multiply_reduce_fusion.1
  727.4 31.9 %psum.102 = f32[]{:T(128)} all-reduce(f32[]{:T(128)} %get-tuple-element.31), channel_id=1, replica_groups=mesh['rows'=16] {'rows'}, use_global_device_ids=true, to_apply=%region_23.0 | all-reduce | flops 1 | bytes 8 | tf_op jit(solution)/shard_map/psum | solution.py:32
  760.6 32.7 %psum.103 = f32[]{:T(128)} all-reduce(f32[]{:T(128)} %get-tuple-element.9), channel_id=1, replica_groups=mesh['rows'=16] {'rows'}, use_global_device_ids=true, to_apply=%region_25.0 | all-reduce | flops 1 | bytes 8 | tf_op jit(solution)/shard_map/psum | solution.py:32
  (71 shorter events, 110.0 us)
Async XLA Ops:
  7.2 75.2 %copy-start = (bf16[32,16,256]{2,1,0:T(8,128)(2,1)S(1)}, bf16[32,16,256]{2,1,0:T(8,128)(2,1)}, u32[]{:S(2)}) copy-start(bf16[32,16,256]{2,1,0:T(8,128)(2,1)} %param.5) | copy-start | bytes 786436
  7.2 69.1 %all-gather.7.cloned.1.call-start = ((), (), s32[]{:S(2)}) async-start(), calls=%async_computation | async-start | bytes 2228224 | tf_op jit(solution)/shard_map/all_gather | solution.py:22
  46.1 156.8 %all-gather.9.cloned.1.call-start = ((), (), s32[]{:S(2)}) async-start(), calls=%async_computation.1 | async-start | bytes 2228224 | tf_op jit(solution)/shard_map/all_gather | solution.py:22
  92.2 7.5 copy-start.1
  172.8 154.6 %all-gather.11.cloned.1.call-start = ((), (), s32[]{:S(2)}) async-start(), calls=%async_computation.2 | async-start | bytes 2228224 | tf_op jit(solution)/shard_map/all_gather | solution.py:22
  297.2 154.5 %all-gather.13.cloned.1.call-start = ((), (), s32[]{:S(2)}) async-start(), calls=%async_computation.3 | async-start | bytes 2228224 | tf_op jit(solution)/shard_map/all_gather | solution.py:22
  421.5 154.5 %all-gather.15.cloned.1.call-start = ((), (), s32[]{:S(2)}) async-start(), calls=%async_computation.4 | async-start | bytes 2228224 | tf_op jit(solution)/shard_map/all_gather | solution.py:22
  545.8 154.7 %all-gather.17.cloned.1.call-start = ((), (), s32[]{:S(2)}) async-start(), calls=%async_computation.5 | async-start | bytes 2228224 | tf_op jit(solution)/shard_map/all_gather | solution.py:22
Sparse Core Ops, SparseCore 0:
  46.3 29.9 all-gather.6
  172.9 29.9 all-gather.8
  297.3 29.9 all-gather.10
  421.7 29.9 all-gather.12
  546.0 29.9 all-gather.14
  670.5 29.9 all-gather.16
where the time goes:
time: 818 us; the launch traced here: 807 us
  blocking collectives  423 us (52%)
  waiting for transfers between devices  168 us (21%)
  local copies, waits for them, and re-layouts  119 us (15%)
  matrix products  56.6 us (7%)
  between operations  23.5 us (3%)
  other arithmetic  15.8 us (2%)
    psum x13, blocking collectives, global_mean(): return lax.psum(jnp.sum(local_val), row_axis) / vec_count  423 us
    all_gather x6, waiting for transfers between devices, matvec(): lax.all_gather(vec_rows.astype(jnp.bfloat16), row_axis, axis=0, tiled=True)  168 us
    dot_general x6, local copies, waits for them, and re-layouts, matvec(): jnp.dot(mid_out, right_flat, preferred_element_type=jnp.float32)  44.5 us
    dot_general x6, matrix products, matvec(): jnp.dot(mid_out, right_flat, preferred_element_type=jnp.float32)  31.9 us
    convert_element_type x6, local copies, waits for them, and re-layouts, matvec(): mid_out.astype(jnp.bfloat16)  26.3 us
    all_gather x6, local copies, waits for them, and re-layouts, matvec(): lax.all_gather(vec_rows.astype(jnp.bfloat16), row_axis, axis=0, tiled=True)  24 us
    unnamed x14, local copies, waits for them, and re-layouts  20.5 us
    dot_general x6, matrix products, matvec(): jnp.einsum('kap,pn->kan', left_rows, flat_in, preferred_element_type=jnp....  17.3 us
  transfers between devices with their start and end apart: 6, of which 6 were waited for; matrix products, arithmetic and copies ran while one was open for 1% of the time, Pallas kernels for 0%

commit v1 on v0

v1 whole, which is shorter than its diff:
```python
import functools

import jax
import jax.numpy as jnp
from jax import lax
from jax.experimental import pallas as pl
from jax.experimental.pallas import tpu as pltpu
from jax.sharding import PartitionSpec as P

NUM_STEPS = 6
MESH = pl.DeviceIdType.MESH
NDEV = 16
PART_EDGES = ((0, 6, 11, 16), (0, 5, 11, 16))
LANES = 128


def kernel(n_count, psi_ref, left_hbm, pair_ref, right_hbm, out_hbm, alpha_ref, beta_ref,
           u_ref, left_ref, right_ref, kron_ref, x_ref, y_ref, sigma_ref, vec_ref, msg_ref, box_ref, bprev_ref,
           ici_send, ici_recv, d2d_send, d2d_recv, sc_send, sc_recv, load_sem, out_sem):
    me = lax.axis_index("rows")
    core = lax.rem(me, 2)
    bits = [lax.rem(me // (2 << d), 2) for d in range(3)]
    partner = me + 1 - 2 * core

    def flip(dev, mask):
        for d in range(3):
            if mask >> d & 1:
                dev = dev + (2 << d) * (1 - 2 * bits[d])
        return dev

    barrier = pltpu.get_barrier_semaphore()
    others = [lax.rem(me + i, NDEV) for i in range(1, NDEV)]
    for dev in others:
        pl.semaphore_signal(barrier, inc=1, device_id=(dev,), device_id_type=MESH)
    loads = [pltpu.make_async_copy(left_hbm, left_ref, load_sem.at[0])]
    for h in range(2):
        loads.append(pltpu.make_async_copy(right_hbm.at[:, h * LANES:(h + 1) * LANES, :], right_ref.at[h], load_sem.at[1 + h]))
    for ld in loads:
        ld.start()

    lane = lax.broadcasted_iota(jnp.int32, (1, LANES), 1)

    def exchange(vals):
        row = jnp.zeros((1, LANES), jnp.float32)
        for t, val in enumerate(vals):
            row = jnp.where(lane == t, val, row)
        msg_ref[...] = row
        box_ref[me] = row
        copies = []
        for i, dev in enumerate(others):
            copies.append(pltpu.make_async_remote_copy(
                src_ref=msg_ref, dst_ref=box_ref.at[me], send_sem=sc_send.at[i], recv_sem=sc_recv.at[NDEV - 2 - i],
                device_id=(dev,), device_id_type=MESH))
        for cp in copies:
            cp.start()
        for i, dev in enumerate(others):
            pltpu.make_async_remote_copy(
                src_ref=msg_ref, dst_ref=box_ref.at[dev], send_sem=sc_send.at[i], recv_sem=sc_recv.at[i],
                device_id=(dev,), device_id_type=MESH).wait_recv()
        for cp in copies:
            cp.wait_send()
        return box_ref[...].reshape(NDEV, LANES)

    def total(arr):
        part = jnp.sum(arr, axis=0)
        part = part[:, :LANES] + part[:, LANES:]
        return jnp.sum(part, axis=(0, 1), keepdims=True)

    exp_row = (lax.broadcasted_iota(jnp.int32, (128, 16), 0) // 8 == lax.broadcasted_iota(jnp.int32, (128, 16), 1)).astype(jnp.bfloat16)
    exp_col = (lax.broadcasted_iota(jnp.int32, (16, 128), 1) // 8 == lax.broadcasted_iota(jnp.int32, (16, 128), 0)).astype(jnp.bfloat16)
    diag = lax.rem(lax.broadcasted_iota(jnp.int32, (128, 128), 0), 8) == lax.rem(lax.broadcasted_iota(jnp.int32, (128, 128), 1), 8)
    wide = jnp.dot(pair_ref[...].reshape(512, 16), exp_col, preferred_element_type=jnp.float32).astype(jnp.bfloat16)
    for k in range(32):
        full = jnp.dot(exp_row, wide[k * 16:(k + 1) * 16, :], preferred_element_type=jnp.float32)
        kron_ref[k] = jnp.where(diag, full, 0.0).astype(jnp.bfloat16)

    pl.semaphore_wait(barrier, NDEV - 1)

    psi = psi_ref[...]
    got = exchange([total(psi * psi)])
    norm = jnp.sqrt(jnp.sum(got[:, 0:1], axis=0, keepdims=True) / n_count)
    vec_ref[0] = psi / norm
    vec_ref[1] = jnp.zeros_like(psi)
    bprev_ref[...] = jnp.zeros_like(bprev_ref)
    for ld in loads:
        ld.wait()

    def region(h, dev, p):
        lo, hi = PART_EDGES[h][p], PART_EDGES[h][p + 1]
        return u_ref.at[h, dev, :, lo * LANES:hi * LANES]

    def dims(p):
        return p, (p + 1) % 3, (p + 2) % 3

    def send_ici(started, h, p, mask, which):
        d = dims(p)[which]
        d0, d1, _ = dims(p)
        slot = {0: which, 1 << d0: 2 + which, 1 << d1: 5, 1 << d0 | 1 << d1: 6}[mask]
        reg = region(h, flip(me, mask), p)
        cp = pltpu.make_async_remote_copy(
            src_ref=reg, dst_ref=reg, send_sem=ici_send.at[h, p, slot], recv_sem=ici_recv.at[h, p, mask ^ (1 << d)],
            device_id=(flip(me, 1 << d),), device_id_type=MESH)
        cp.start()
        started.append(cp)

    def send_d2d(started, h, p, mask):
        reg = region(h, flip(me, mask), p)
        cp = pltpu.make_async_remote_copy(
            src_ref=reg, dst_ref=reg, send_sem=d2d_send.at[h, p, mask], recv_sem=d2d_recv.at[h, p, mask],
            device_id=(partner,), device_id_type=MESH)
        cp.start()
        started.append(cp)

    def wait_ici(h, p, mask):
        reg = region(h, flip(me, mask), p)
        pltpu.make_async_remote_copy(
            src_ref=reg, dst_ref=reg, send_sem=ici_send.at[h, p, 0], recv_sem=ici_recv.at[h, p, mask],
            device_id=(partner,), device_id_type=MESH).wait_recv()

    def wait_d2d(h, p, mask):
        reg = region(h, flip(partner, mask), p)
        pltpu.make_async_remote_copy(
            src_ref=reg, dst_ref=reg, send_sem=d2d_send.at[h, p, mask], recv_sem=d2d_recv.at[h, p, mask],
            device_id=(partner,), device_id_type=MESH).wait_recv()

    def apply_half(h):
        left = left_ref[...].reshape(512, 256)
        for rp in range(8):
            cols = u_ref[h, :, :, rp * 256:(rp + 1) * 256].reshape(256, 256)
            res = jnp.dot(left, cols, preferred_element_type=jnp.float32)
            lo = res[:, :LANES].reshape(64, 8, LANES)
            hi = res[:, LANES:].reshape(64, 8, LANES)
            x_ref[:, rp * 16:(rp + 1) * 16, :] = jnp.concatenate([lo, hi], axis=1).astype(jnp.bfloat16)
        for k in range(32):
            rhs = jnp.concatenate([x_ref[2 * k], x_ref[2 * k + 1]], axis=1)
            res = jnp.dot(kron_ref[k], rhs, preferred_element_type=jnp.float32).astype(jnp.bfloat16)
            y_ref[0:128, k * LANES:(k + 1) * LANES] = res[:, :LANES]
            y_ref[128:256, k * LANES:(k + 1) * LANES] = res[:, LANES:]
        return jnp.dot(y_ref[...], right_ref[h].reshape(4096, 256), preferred_element_type=jnp.float32).reshape(32, 8, 256)

    def out_copy(slot, j):
        return pltpu.make_async_copy(vec_ref.at[slot], out_hbm.at[j], out_sem.at[slot])

    def step(j, carry):
        cur = lax.rem(j, 2)
        prv = 1 - cur
        vec = vec_ref[cur]
        for h in range(2):
            for r in range(16):
                tile = jnp.concatenate([vec[r, :, h * LANES:(h + 1) * LANES], vec[16 + r, :, h * LANES:(h + 1) * LANES]], axis=0)
                u_ref[h, me, :, r * LANES:(r + 1) * LANES] = tile.astype(jnp.bfloat16)
        started = []
        for which in range(3):
            for p in range(3):
                send_ici(started, 0, p, 0, which)
        for p in range(3):
            send_ici(started, 1, p, 0, 0)
        for h in range(2):
            for p in range(3):
                send_d2d(started, h, p, 0)
        out_copy(cur, j).start()
        prev = vec_ref[prv]
        beta_prev = bprev_ref[0:1, 0:1]
        s_vv = total(vec * vec)
        s_pv = total(prev * vec)

        def first_hop(h):
            for p in range(3):
                m = 1 << dims(p)[0]
                wait_ici(h, p, m)
                send_ici(started, h, p, m, 1)
                send_ici(started, h, p, m, 2)
                send_d2d(started, h, p, m)

        def second_hop(h, mask_of):
            for p in range(3):
                m = mask_of(*dims(p))
                wait_ici(h, p, m)
                send_ici(started, h, p, m, 2)
                send_d2d(started, h, p, m)

        def last_hop(h, mask_of):
            for p in range(3):
                m = mask_of(*dims(p))
                wait_ici(h, p, m)
                send_d2d(started, h, p, m)

        first_hop(0)
        for which in (1, 2):
            for p in range(3):
                send_ici(started, 1, p, 0, which)
        second_hop(0, lambda a, b, c: 1 << b)
        last_hop(0, lambda a, b, c: 1 << c)
        first_hop(1)
        second_hop(0, lambda a, b, c: 1 << a | 1 << b)
        second_hop(1, lambda a, b, c: 1 << b)
        last_hop(0, lambda a, b, c: 1 << a | 1 << c)
        last_hop(0, lambda a, b, c: 1 << b | 1 << c)
        last_hop(1, lambda a, b, c: 1 << c)
        second_hop(1, lambda a, b, c: 1 << a | 1 << b)
        last_hop(0, lambda a, b, c: 7)
        for p in range(3):
            for m in range(8):
                wait_d2d(0, p, m)
        sigma_ref[...] = apply_half(0)
        last_hop(1, lambda a, b, c: 1 << a | 1 << c)
        last_hop(1, lambda a, b, c: 1 << b | 1 << c)
        last_hop(1, lambda a, b, c: 7)
        for p in range(3):
            for m in range(8):
                wait_d2d(1, p, m)
        sigma = sigma_ref[...] + apply_half(1)
        sigma_ref[...] = sigma
        for cp in started:
            cp.wait_send()

        s_sv = total(sigma * vec)
        has = s_vv > 0.0
        proj = jnp.where(has, (s_sv - beta_prev * s_pv) / jnp.where(has, s_vv, 1.0), 0.0)
        res = sigma - beta_prev * prev - proj * vec
        got = exchange([s_sv, total(res * res), total(res * vec), s_vv, proj])
        alpha = jnp.sum(got[:, 0:1], axis=0, keepdims=True) / n_count
        shift = got[:, 4:5] - alpha
        sq = got[:, 1:2] + 2.0 * (shift * got[:, 2:3]) + (shift * got[:, 3:4]) * shift
        beta = jnp.sqrt(jnp.sum(sq, axis=0, keepdims=True) / n_count)
        new = (sigma_ref[...] - alpha * vec_ref[cur] - beta_prev * vec_ref[prv]) / beta

        @pl.when(j > 0)
        def _():
            out_copy(prv, j - 1).wait()

        vec_ref[prv] = new
        bprev_ref[...] = jnp.broadcast_to(beta, bprev_ref.shape)
        alpha_ref[j] = alpha[0, 0]
        beta_ref[j] = beta[0, 0]
        return carry

    lax.fori_loop(0, NUM_STEPS, step, 0)
    last = out_copy(NUM_STEPS % 2, NUM_STEPS)
    last.start()
    out_copy((NUM_STEPS - 1) % 2, NUM_STEPS - 1).wait()
    last.wait()


def solution(mesh):
    def local_run(wave_rows, left_rows, op_pair, right_env):
        psi = wave_rows.reshape(2, 8, 16, 256).transpose(0, 2, 1, 3).reshape(32, 8, 256)
        vmem = pl.BlockSpec(memory_space=pltpu.VMEM)
        smem = pl.BlockSpec(memory_space=pltpu.SMEM)
        hbm = pl.BlockSpec(memory_space=pl.ANY)
        vecs, alpha, beta = pl.pallas_call(
            functools.partial(kernel, float(wave_rows.size * NDEV)),
            out_shape=(jax.ShapeDtypeStruct((NUM_STEPS + 1, 32, 8, 256), jnp.float32),
                       jax.ShapeDtypeStruct((NUM_STEPS,), jnp.float32),
                       jax.ShapeDtypeStruct((NUM_STEPS,), jnp.float32)),
            in_specs=[vmem, hbm, vmem, hbm],
            out_specs=(hbm, smem, smem),
            scratch_shapes=[
                pltpu.VMEM((2, NDEV, 16, 2048), jnp.bfloat16),
                pltpu.VMEM((32, 16, 256), jnp.bfloat16),
                pltpu.VMEM((2, 32, LANES, 256), jnp.bfloat16),
                pltpu.VMEM((32, 128, 128), jnp.bfloat16),
                pltpu.VMEM((64, 128, LANES), jnp.bfloat16),
                pltpu.VMEM((256, 4096), jnp.bfloat16),
                pltpu.VMEM((32, 8, 256), jnp.float32),
                pltpu.VMEM((2, 32, 8, 256), jnp.float32),
                pltpu.VMEM((1, LANES), jnp.float32),
                pltpu.VMEM((NDEV, 1, LANES), jnp.float32),
                pltpu.VMEM((8, LANES), jnp.float32),
                pltpu.SemaphoreType.DMA((2, 3, 7)),
                pltpu.SemaphoreType.DMA((2, 3, 8)),
                pltpu.SemaphoreType.DMA((2, 3, 8)),
                pltpu.SemaphoreType.DMA((2, 3, 8)),
                pltpu.SemaphoreType.DMA((NDEV - 1,)),
                pltpu.SemaphoreType.DMA((NDEV - 1,)),
                pltpu.SemaphoreType.DMA((3,)),
                pltpu.SemaphoreType.DMA((2,)),
            ],
            compiler_params=pltpu.CompilerParams(collective_id=0, has_side_effects=True, vmem_limit_bytes=48 * 1024 * 1024),
        )(psi, left_rows, op_pair, right_env)
        vecs = vecs.reshape(7, 2, 16, 8, 256).transpose(0, 1, 3, 2, 4).reshape(7, 16, 4, 4, 256)
        return vecs, alpha, beta

    return jax.shard_map(local_run, mesh=mesh, in_specs=(P("rows"), P(None, "rows"), P(), P()), out_specs=(P(None, "rows"), P(), P()), check_vma=False)
```

time: 818 us -> 145 us (0.18); the launches traced: 807 us -> 145 us
  blocking collectives: 423 us -> 0 us
  waiting for transfers between devices: 168 us -> 0 us
  Pallas kernels: 0 us -> 138 us
  local copies, waits for them, and re-layouts: 119 us -> 6.49 us
  matrix products: 56.6 us -> 0 us
  between operations: 23.5 us -> 0.67 us
  other arithmetic: 15.8 us -> 0 us
    psum x13 -> x0, blocking collectives: 423 us -> none  [global_mean(): return lax.psum(jnp.sum(local_val), row_axis) / vec_count]
    all_gather x6 -> x0, waiting for transfers between devices: 168 us -> none  [matvec(): lax.all_gather(vec_rows.astype(jnp.bfloat16), row_axis, axis=0, tiled=True)]
    pallas_call x0 -> x1, Pallas kernels: none -> 138 us  [local_run(): pl.pallas_call(functools.partial(kernel, float(wave_rows.size * NDEV)), o...]
    dot_general x18 -> x0, matrix products: 56.6 us -> none  [the longest x6 31.9 us: matvec(): jnp.dot(mid_out, right_flat, preferred_element_type=jnp.float32)]
    dot_general x6 -> x0, local copies, waits for them, and re-layouts: 44.5 us -> none  [matvec(): jnp.dot(mid_out, right_flat, preferred_element_type=jnp.float32)]
    convert_element_type x6 -> x0, local copies, waits for them, and re-layouts: 26.3 us -> none  [matvec(): mid_out.astype(jnp.bfloat16)]
    all_gather x6 -> x0, local copies, waits for them, and re-layouts: 24 us -> none  [matvec(): lax.all_gather(vec_rows.astype(jnp.bfloat16), row_axis, axis=0, tiled=True)]
    unnamed x14 -> x5, local copies, waits for them, and re-layouts: 20.5 us -> 2.96 us
  transfers between devices with their start and end apart: 6 -> 0, of which waited for: 6 -> 0; matrix products, arithmetic and copies ran while one was open for 1% -> 0% of each run, Pallas kernels for 0% -> 0%
where the time goes in v1:
time: 145 us
  Pallas kernels  138 us (95%)
  local copies, waits for them, and re-layouts  6.49 us (4%)
    pallas_call x1, Pallas kernels, local_run(): pl.pallas_call(functools.partial(kernel, float(wave_rows.size * NDEV)), o...  138 us
    unnamed x5, local copies, waits for them, and re-layouts  2.96 us

profile of v1, /device:TPU:0, one launch (start us, length us, event | category | flops | bytes accessed | tf_op | source)
XLA Modules:
  0.0 145.1 jit_solution(18350129585200788521)
XLA Ops:
  0.6 1.0 copy.8.pair_ref
  1.6 1.0 reshape.18
  2.7 0.2 copy.7
  2.8 0.0 copy-start
  2.9 0.9 copy-done
  3.8 138.0 %shard_map.67 = (f32[7,32,8,256]{3,2,1,0:T(8,128)S(1)}, f32[6]{0:T(128)S(1)}, f32[6]{0:T(128)S(1)}) custom-call(f32[32,8,256]{2,1,0:T(8,128)S(1)} %bitcast.9, bf16[32,16,256]{2,1,0:T(8,128)(2,1)S(1)} %copy-done, bf16[32,16,16]{2,1,0:T(8,128)(2,1)S(1)} %copy.8.pair_ref, bf16[32,256,256]{2,1,0:T(8,128)(2,1)} %right_hbm.1), custom_call_target="tpu_custom_call" | custom-call | tf_op jit(solution)/shard_map/pallas_call | solution.py:251
  141.8 0.6 copy.9
  142.3 1.8 %reshape.21 = f32[7,16,4,4,256]{4,3,2,1,0:T(4,128)} reshape(f32[7,2,8,16,256]{4,3,2,1,0:T(8,128)S(1)} %copy.9) | data formatting | bytes 3670016 | tf_op jit(solution)/shard_map/reshape | solution.py:281
  144.1 0.5 copy.12
  144.6 0.5 copy.13
Async XLA Ops:
  2.8 1.0 copy-start
